TPU v7x, 128 devices: a whole 4x4x4 slice. The times are simulated.
128 devices in a mesh: grp: 4 (over z_lo, core), tile: 32 (over x, z_hi, y).
Axes of the slice: x: 4, y: 4, z: 4 (z_hi: 2, z_lo: 2; z = z_hi * 2 + z_lo), core: 2. Of those that a mesh axis runs over, the one named last changes fastest.
Arguments:
- amplitudes: bfloat16 [160, 4, 983040], P(None, None, ('grp', 'tile')), may hold values from -6 to 6
- w_vvvo: bfloat16 [1024, 983040], P(None, ('grp', 'tile')), may hold values from -0.0234375 to 0.0234375
- pair_mask: int32 [4096], P(('grp', 'tile')), may hold values from 0 to 1, as said below
- owner_map: int32 [32], replicated, may hold values from 0 to 31, each once
Outputs:
- sigma_one: float32 [160, 4, 1024], P('tile', None, 'grp')
Inputs may be any that keep to these rules, and one draw needn't show every extreme that they name: `pair_mask`: in each aligned block of 32 pairs at most 24 are 1 and at least one is; some block has exactly 24 and some block exactly one. `owner_map`: a permutation of the row blocks.
All inputs are finite; a program needn't handle non-finite values.
Results may differ from a plain program's by a relative error of at most 0.0003.
Values sent between devices are 32-bit elements; how exact they have to be, the bound alone decides.
A program may use at most 128 MiB of HBM per device.

v0:
```python
import jax
import jax.numpy as jnp
from jax import lax
from jax.sharding import PartitionSpec as P


def split_up(shard, dim, size):
    before, after = (shard.shape[:dim], shard.shape[dim + 1 :])
    return jnp.moveaxis(shard.reshape(*before, size, -1, *after), dim, 0)


def sent_and_summed(shard, axis, dim):
    parts = split_up(shard, dim, lax.axis_size(axis))
    arrived = lax.all_to_all(parts, axis, split_axis=0, concat_axis=0, tiled=True)
    return arrived.sum(axis=0)


def full_product(amp_flat, weights, mask_cols):
    masked = amp_flat * mask_cols
    return lax.dot_general(
        weights, masked, (((1,), (1,)), ((), ())), preferred_element_type=jnp.float32
    )


def shards(amplitudes, w_vvvo, pair_mask, owner_map):
    occ_total, root_count, pair_cols = amplitudes.shape
    virt_total = w_vvvo.shape[0]
    tile_count = lax.axis_size("tile")
    occ_rows = occ_total // tile_count
    pair_count = pair_mask.shape[0]
    occ_width = pair_cols // pair_count
    mask_cols = jnp.repeat(pair_mask.astype(jnp.bfloat16), occ_width, total_repeat_length=pair_cols)
    virt_rows = virt_total // lax.axis_size("grp")
    amp_flat = amplitudes.reshape(occ_total * root_count, pair_cols)
    term = full_product(amp_flat, w_vvvo, mask_cols)
    term = term.reshape(virt_rows * lax.axis_size("grp"), tile_count, occ_rows * root_count)
    owned = sent_and_summed(
        jnp.take(term, owner_map, axis=1).reshape(
            virt_rows * lax.axis_size("grp"), occ_total * root_count
        ),
        "grp",
        0,
    )
    partial_value = sent_and_summed(owned, "tile", 1)
    sigma_one = jnp.transpose(partial_value.reshape(virt_rows, occ_rows, root_count), (1, 2, 0))
    return sigma_one


def solution(mesh):
    return jax.shard_map(
        shards,
        mesh=mesh,
        in_specs=(
            P(None, None, ("grp", "tile")),
            P(None, ("grp", "tile")),
            P(("grp", "tile")),
            P(),
        ),
        out_specs=P("tile", None, "grp"),
        check_vma=False,
    )
```

profile of v0, /device:TPU:0, one launch (start us, length us, event | category | flops | bytes accessed | tf_op | source)
XLA Modules:
  0.0 125.7 jit_solution(4318091118811727333)
XLA Ops:
  0.0 0.7 convert_element_type.3
  0.7 0.7 fusion.6
  1.4 0.7 fusion.7
  2.1 0.7 compare_select_fusion
  2.7 0.7 compare_and_fusion
  3.4 0.0 copy-start.2
  3.4 0.0 copy-start.3
  3.4 0.0 copy-start.4
  3.4 0.0 copy-start.5
  3.5 0.0 copy-start.6
  3.5 0.0 copy-start.7
  3.5 0.0 copy-start.8
  3.5 0.0 copy-start.9
  3.5 0.0 copy-start.10
  3.5 0.0 copy-start.11
  3.5 0.0 copy-start.12
  3.5 0.0 copy-start.13
  3.6 0.0 copy-start.14
  3.6 0.0 copy-start.15
  3.6 0.0 copy-start.16
  3.6 0.0 copy-start.17
  3.6 0.0 copy-start.18
  3.6 0.0 copy-start.19
  3.6 0.0 copy-start.20
  3.6 0.0 copy-start.21
  3.7 0.0 copy-start.22
  3.7 0.0 copy-start.23
  3.7 0.0 copy-start.24
  3.7 0.0 copy-start.25
  3.7 0.0 copy-start.26
  3.7 0.0 copy-start.27
  3.7 0.0 copy-start.28
  3.8 0.0 copy-start.29
  3.8 0.0 copy-start.30
  3.8 13.3 %reshape.107 = bf16[640,7680]{1,0:T(8,128)(2,1)} reshape(bf16[160,4,7680]{2,1,0:T(4,128)(2,1)} %param.6) | data formatting | bytes 19660800 | tf_op jit(solution)/shard_map/reshape | solution.py:34
  17.1 0.0 copy-done
  17.1 0.0 copy-done.1
  17.1 0.0 copy-done.2
  17.1 0.0 copy-done.3
  17.1 0.0 copy-done.4
  17.1 0.0 copy-done.5
  17.2 0.0 copy-done.6
  17.2 0.0 copy-done.7
  17.2 0.0 copy-done.8
  17.2 0.0 copy-done.9
  17.2 0.0 copy-done.10
  17.2 0.0 copy-done.11
  17.2 0.0 copy-done.12
  17.2 0.0 copy-done.13
  17.4 19.7 %select_select_fusion = bf16[7680]{0:T(1024)(128)(2,1)S(1)} fusion(pred[7680]{0:T(1024)(128)(4,1)S(1)} %copy-done, pred[7680]{0:T(1024)(128)(4,1)S(1)} %copy-done.1, pred[7680]{0:T(1024)(128)(4,1)S(1)} %copy-done.2, pred[7680]{0:T(1024)(128)(4,1)S(1)} %copy-done.3, pred[7680]{0:T(1024)(128)(4,1)S(1)} %copy-done.4, pred[7680]{0:T(1024)(128)(4,1)S(1)} %copy-done.5, ...), kind=kLoop, calls=%fused_computation.6 | loop fusion | flops 238080 | bytes 253504 | tf_op jit(solution)/shard_map/jit(_take)/gather | solution.py:32
  37.1 16.8 %fusion.3 = f32[1024,640]{0,1:T(8,128)} fusion(bf16[1024,7680]{1,0:T(8,128)(2,1)} %param.7, bf16[640,7680]{1,0:T(8,128)(2,1)} %reshape.107, bf16[7680]{0:T(1024)(128)(2,1)S(1)} %select_select_fusion), kind=kOutput, calls=%fused_computation.4 | convolution fusion | flops 10071244800 | bytes 28195840 | tf_op jit(solution)/shard_map/dot_general | solution.py:20
  53.9 2.5 %reshape.108 = f32[1024,32,20]{0,2,1:T(8,128)S(1)} reshape(f32[1024,640]{0,1:T(8,128)} %fusion.3) | data formatting | bytes 5242880 | tf_op jit(solution)/shard_map/reshape | solution.py:36
  56.4 2.4 %gather_fusion = f32[32,1024,20]{1,2,0:T(8,128)} fusion(f32[1024,32,20]{0,2,1:T(8,128)S(1)} %reshape.108, s32[1024]{0:T(1024)S(1)} %pad_clamp_fusion), kind=kCustom, calls=%fused_computation | custom fusion | bytes 5243008 | tf_op jit(solution)/shard_map/jit(_take)/gather | solution.py:38
  58.8 3.2 %gather.12 = f32[4,256,640]{1,0,2:T(4,128)S(1)} reshape(f32[1024,32,20]{0,2,1:T(8,128)} %bitcast.46) | data formatting | bytes 5242880 | tf_op jit(solution)/shard_map/jit(_take)/gather | solution.py:38
  62.0 0.1 broadcast_in_dim.25
  62.1 0.1 broadcast_in_dim.26
  62.2 2.3 %broadcast_select_fusion = f32[4,256,640]{1,0,2:T(4,128)S(1)} fusion(f32[4,256,640]{1,0,2:T(4,128)S(1)} %gather.12, pred[640]{0:T(1024)(128)(4,1)S(1)} %broadcast_in_dim.26), kind=kLoop, calls=%fused_computation.5 | loop fusion | flops 655360 | bytes 5243520 | tf_op jit(solution)/shard_map/jit(_take)/select_n | solution.py:38
  64.5 0.5 copy.5
  65.0 34.4 %all_to_all.10 = f32[4,256,640]{1,2,0:T(8,128)S(1)} all-to-all(f32[4,256,640]{1,2,0:T(8,128)S(1)} %copy.5), channel_id=1, replica_groups=mesh['grp'=4,'tile'=32] {'grp'}, dimensions={0} | all-to-all | bytes 5242880 | tf_op jit(solution)/shard_map/all_to_all | solution.py:14
  99.4 0.2 reduce_sum.18
  99.7 0.1 reshape.109
  99.7 25.3 %all_to_all.11 = f32[32,256,20]{1,2,0:T(8,128)S(1)} all-to-all(f32[32,256,20]{1,2,0:T(8,128)S(1)} %bitcast.47), channel_id=1, replica_groups=mesh['grp'=4,'tile'=32] {'tile'}, dimensions={0} | all-to-all | bytes 1310720 | tf_op jit(solution)/shard_map/all_to_all | solution.py:14
  125.0 0.1 reduce_sum.19
  125.1 0.6 reshape.110
  (20 shorter events, 0.0 us)
Async XLA Ops:
  3.4 13.7 %copy-start = (pred[7680]{0:T(1024)(128)(4,1)S(1)}, pred[7680]{0:T(1024)(128)(4,1)}, u32[]{:S(2)}) copy-start(pred[7680]{0:T(1024)(128)(4,1)} %constant.152) | copy-start | bytes 23044
  3.4 13.7 %copy-start.1 = (pred[7680]{0:T(1024)(128)(4,1)S(1)}, pred[7680]{0:T(1024)(128)(4,1)}, u32[]{:S(2)}) copy-start(pred[7680]{0:T(1024)(128)(4,1)} %constant.153) | copy-start | bytes 23044
  3.4 13.7 %copy-start.2 = (pred[7680]{0:T(1024)(128)(4,1)S(1)}, pred[7680]{0:T(1024)(128)(4,1)}, u32[]{:S(2)}) copy-start(pred[7680]{0:T(1024)(128)(4,1)} %constant.154) | copy-start | bytes 23044
  3.4 13.7 %copy-start.3 = (pred[7680]{0:T(1024)(128)(4,1)S(1)}, pred[7680]{0:T(1024)(128)(4,1)}, u32[]{:S(2)}) copy-start(pred[7680]{0:T(1024)(128)(4,1)} %constant.155) | copy-start | bytes 23044
  3.4 13.7 %copy-start.4 = (pred[7680]{0:T(1024)(128)(4,1)S(1)}, pred[7680]{0:T(1024)(128)(4,1)}, u32[]{:S(2)}) copy-start(pred[7680]{0:T(1024)(128)(4,1)} %constant.156) | copy-start | bytes 23044
  3.4 13.7 %copy-start.5 = (pred[7680]{0:T(1024)(128)(4,1)S(1)}, pred[7680]{0:T(1024)(128)(4,1)}, u32[]{:S(2)}) copy-start(pred[7680]{0:T(1024)(128)(4,1)} %constant.157) | copy-start | bytes 23044
  3.5 13.7 %copy-start.6 = (pred[7680]{0:T(1024)(128)(4,1)S(1)}, pred[7680]{0:T(1024)(128)(4,1)}, u32[]{:S(2)}) copy-start(pred[7680]{0:T(1024)(128)(4,1)} %constant.158) | copy-start | bytes 23044
  3.5 13.7 %copy-start.7 = (pred[7680]{0:T(1024)(128)(4,1)S(1)}, pred[7680]{0:T(1024)(128)(4,1)}, u32[]{:S(2)}) copy-start(pred[7680]{0:T(1024)(128)(4,1)} %constant.159) | copy-start | bytes 23044
  3.5 13.7 %copy-start.8 = (pred[7680]{0:T(1024)(128)(4,1)S(1)}, pred[7680]{0:T(1024)(128)(4,1)}, u32[]{:S(2)}) copy-start(pred[7680]{0:T(1024)(128)(4,1)} %constant.160) | copy-start | bytes 23044
  3.5 13.7 %copy-start.9 = (pred[7680]{0:T(1024)(128)(4,1)S(1)}, pred[7680]{0:T(1024)(128)(4,1)}, u32[]{:S(2)}) copy-start(pred[7680]{0:T(1024)(128)(4,1)} %constant.161) | copy-start | bytes 23044
  3.5 13.7 %copy-start.10 = (pred[7680]{0:T(1024)(128)(4,1)S(1)}, pred[7680]{0:T(1024)(128)(4,1)}, u32[]{:S(2)}) copy-start(pred[7680]{0:T(1024)(128)(4,1)} %constant.162) | copy-start | bytes 23044
  3.5 13.7 %copy-start.11 = (pred[7680]{0:T(1024)(128)(4,1)S(1)}, pred[7680]{0:T(1024)(128)(4,1)}, u32[]{:S(2)}) copy-start(pred[7680]{0:T(1024)(128)(4,1)} %constant.163) | copy-start | bytes 23044
  3.5 13.7 %copy-start.12 = (pred[7680]{0:T(1024)(128)(4,1)S(1)}, pred[7680]{0:T(1024)(128)(4,1)}, u32[]{:S(2)}) copy-start(pred[7680]{0:T(1024)(128)(4,1)} %constant.164) | copy-start | bytes 23044
  3.5 13.7 %copy-start.13 = (pred[7680]{0:T(1024)(128)(4,1)S(1)}, pred[7680]{0:T(1024)(128)(4,1)}, u32[]{:S(2)}) copy-start(pred[7680]{0:T(1024)(128)(4,1)} %constant.165) | copy-start | bytes 23044
  3.6 13.7 %copy-start.14 = (pred[7680]{0:T(1024)(128)(4,1)S(1)}, pred[7680]{0:T(1024)(128)(4,1)}, u32[]{:S(2)}) copy-start(pred[7680]{0:T(1024)(128)(4,1)} %constant.166) | copy-start | bytes 23044
  3.6 13.7 %copy-start.15 = (pred[7680]{0:T(1024)(128)(4,1)S(1)}, pred[7680]{0:T(1024)(128)(4,1)}, u32[]{:S(2)}) copy-start(pred[7680]{0:T(1024)(128)(4,1)} %constant.167) | copy-start | bytes 23044
  3.6 13.7 %copy-start.16 = (pred[7680]{0:T(1024)(128)(4,1)S(1)}, pred[7680]{0:T(1024)(128)(4,1)}, u32[]{:S(2)}) copy-start(pred[7680]{0:T(1024)(128)(4,1)} %constant.168) | copy-start | bytes 23044
  3.6 13.7 %copy-start.17 = (pred[7680]{0:T(1024)(128)(4,1)S(1)}, pred[7680]{0:T(1024)(128)(4,1)}, u32[]{:S(2)}) copy-start(pred[7680]{0:T(1024)(128)(4,1)} %constant.169) | copy-start | bytes 23044
  3.6 13.7 %copy-start.18 = (pred[7680]{0:T(1024)(128)(4,1)S(1)}, pred[7680]{0:T(1024)(128)(4,1)}, u32[]{:S(2)}) copy-start(pred[7680]{0:T(1024)(128)(4,1)} %constant.170) | copy-start | bytes 23044
  3.6 13.7 %copy-start.19 = (pred[7680]{0:T(1024)(128)(4,1)S(1)}, pred[7680]{0:T(1024)(128)(4,1)}, u32[]{:S(2)}) copy-start(pred[7680]{0:T(1024)(128)(4,1)} %constant.171) | copy-start | bytes 23044
  3.6 13.7 %copy-start.20 = (pred[7680]{0:T(1024)(128)(4,1)S(1)}, pred[7680]{0:T(1024)(128)(4,1)}, u32[]{:S(2)}) copy-start(pred[7680]{0:T(1024)(128)(4,1)} %constant.172) | copy-start | bytes 23044
  3.6 13.7 %copy-start.21 = (pred[7680]{0:T(1024)(128)(4,1)S(1)}, pred[7680]{0:T(1024)(128)(4,1)}, u32[]{:S(2)}) copy-start(pred[7680]{0:T(1024)(128)(4,1)} %constant.173) | copy-start | bytes 23044
  3.7 13.7 %copy-start.22 = (pred[7680]{0:T(1024)(128)(4,1)S(1)}, pred[7680]{0:T(1024)(128)(4,1)}, u32[]{:S(2)}) copy-start(pred[7680]{0:T(1024)(128)(4,1)} %constant.174) | copy-start | bytes 23044
  3.7 13.7 %copy-start.23 = (pred[7680]{0:T(1024)(128)(4,1)S(1)}, pred[7680]{0:T(1024)(128)(4,1)}, u32[]{:S(2)}) copy-start(pred[7680]{0:T(1024)(128)(4,1)} %constant.175) | copy-start | bytes 23044
  3.7 13.7 %copy-start.24 = (pred[7680]{0:T(1024)(128)(4,1)S(1)}, pred[7680]{0:T(1024)(128)(4,1)}, u32[]{:S(2)}) copy-start(pred[7680]{0:T(1024)(128)(4,1)} %constant.176) | copy-start | bytes 23044
  3.7 13.6 %copy-start.25 = (pred[7680]{0:T(1024)(128)(4,1)S(1)}, pred[7680]{0:T(1024)(128)(4,1)}, u32[]{:S(2)}) copy-start(pred[7680]{0:T(1024)(128)(4,1)} %constant.177) | copy-start | bytes 23044
  3.7 13.6 %copy-start.26 = (pred[7680]{0:T(1024)(128)(4,1)S(1)}, pred[7680]{0:T(1024)(128)(4,1)}, u32[]{:S(2)}) copy-start(pred[7680]{0:T(1024)(128)(4,1)} %constant.178) | copy-start | bytes 23044
  3.7 13.6 %copy-start.27 = (pred[7680]{0:T(1024)(128)(4,1)S(1)}, pred[7680]{0:T(1024)(128)(4,1)}, u32[]{:S(2)}) copy-start(pred[7680]{0:T(1024)(128)(4,1)} %constant.179) | copy-start | bytes 23044
  3.7 13.6 %copy-start.28 = (pred[7680]{0:T(1024)(128)(4,1)S(1)}, pred[7680]{0:T(1024)(128)(4,1)}, u32[]{:S(2)}) copy-start(pred[7680]{0:T(1024)(128)(4,1)} %constant.180) | copy-start | bytes 23044
  3.8 13.6 %copy-start.29 = (pred[7680]{0:T(1024)(128)(4,1)S(1)}, pred[7680]{0:T(1024)(128)(4,1)}, u32[]{:S(2)}) copy-start(pred[7680]{0:T(1024)(128)(4,1)} %constant.181) | copy-start | bytes 23044
  3.8 13.6 %copy-start.30 = (pred[7680]{0:T(1024)(128)(4,1)S(1)}, pred[7680]{0:T(1024)(128)(4,1)}, u32[]{:S(2)}) copy-start(pred[7680]{0:T(1024)(128)(4,1)} %constant.182) | copy-start | bytes 23044
where the time goes:
time: 127 us; the launch traced here: 126 us
  blocking collectives  59.6 us (47%)
  local copies, waits for them, and re-layouts  24.5 us (19%)
  other arithmetic  24.3 us (19%)
  matrix products  16.8 us (13%)
    all_to_all x2, blocking collectives, sent_and_summed(): lax.all_to_all(parts, axis, split_axis=0, concat_axis=0, tiled=True)  59.6 us
    gather x1, other arithmetic, shards(): jnp.repeat(pair_mask.astype(jnp.bfloat16), occ_width, total_repeat_length...  19.7 us
    dot_general x1, matrix products, full_product(): lax.dot_general(weights, masked, (((1,), (1,)), ((), ())), preferred_elem...  16.8 us
    reshape x1, local copies, waits for them, and re-layouts, shards(): amp_flat = amplitudes.reshape(occ_total * root_count, pair_cols)  13.3 us
    gather x2, local copies, waits for them, and re-layouts, shards(): jnp.take(term, owner_map, axis=1)  5.6 us
    select_n x2, other arithmetic, shards(): jnp.take(term, owner_map, axis=1)  2.97 us

commit v1 on v0

v1 whole, which is shorter than its diff:
```python
import jax
import jax.numpy as jnp
from jax import lax
from jax.experimental import pallas as pl
from jax.experimental.pallas import tpu as pltpu
from jax.sharding import PartitionSpec as P

MESH = pl.DeviceIdType.MESH
F32 = jnp.float32
BF16 = jnp.bfloat16

NK = 15
KC = 512
OCC = 240
AHEAD = 4
ROWS = (8, 8, 4)
BASE = (0, 32, 64)
LANES = 128


def kernel(
    pm, om, a_hbm, w_hbm, out, a_raw, a2, wb, sib0, sib1, own0, own1, prt0, prt1, s0, s1, s2, r10, r11, r12,
    r20, r21, r22, r30, r31, r32, t10, t11, t12, t20, t21, t22,
    sem_a, sem_w, dsend, drecv, ssend, srecv,
):
    grp = lax.axis_index("grp")
    tile = lax.axis_index("tile")
    core = lax.rem(grp, 2)
    z_lo = grp // 2
    x = tile // 8
    z_hi = lax.rem(tile // 4, 2)
    y = lax.rem(tile, 4)
    z = z_hi * 2 + z_lo
    place = (x, y, z)
    sib, own, prt = (sib0, sib1), (own0, own1), (prt0, prt1)
    S = (s0, s1, s2)
    R = ((r10, r11, r12), (r20, r21, r22), (r30, r31, r32))
    T = ((t10, t11, t12), (t20, t21, t22))

    def peer(axis, d):
        to = [x, y, z]
        to[axis] = lax.rem(to[axis] + d, 4)
        px, py, pz = to
        return (lax.rem(pz, 2) * 2 + core, (px * 2 + pz // 2) * 4 + py)

    sibling = (z_lo * 2 + 1 - core, tile)

    barrier = pltpu.get_barrier_semaphore()
    pl.semaphore_signal(barrier, inc=1, device_id=sibling, device_id_type=MESH)
    for axis in range(3):
        for d in (1, 2, 3):
            pl.semaphore_signal(barrier, inc=1, device_id=peer(axis, d), device_id_type=MESH)

    def copy_a(k):
        return pltpu.make_async_copy(
            a_hbm.at[:, :, pl.ds(pl.multiple_of(k * KC, KC), KC)], a_raw.at[k], sem_a.at[k]
        )

    def copy_w(h, s, k):
        owner = core if s == 1 else 1 - core
        return pltpu.make_async_copy(
            w_hbm.at[:, owner, h, :, pl.ds(pl.multiple_of(k * KC, KC), KC)],
            wb.at[h, s, k],
            sem_w.at[h, s, k],
        )

    def start_first(k):
        copy_a(k).start()
        copy_w(0, 0, k).start()
        copy_w(0, 1, k).start()

    def wait_first(k):
        copy_a(k).wait()
        copy_w(0, 0, k).wait()
        copy_w(0, 1, k).wait()

    def prepare(k):
        first = (k * KC) // OCC
        lane = lax.broadcasted_iota(jnp.int32, (1, KC), 1)
        keep = [pm[jnp.minimum(first + j, 31)] for j in range(4)]
        edge = [OCC * (first + j + 1) - k * KC for j in range(3)]
        mask = jnp.where(
            lane < edge[0],
            keep[0],
            jnp.where(lane < edge[1], keep[1], jnp.where(lane < edge[2], keep[2], keep[3])),
        )
        mask = mask.astype(F32).astype(BF16)
        v = a_raw[k].reshape(32, 5, 4, KC)
        a2[k, 0:256] = v[:, 0:2].reshape(256, KC) * mask
        a2[k, 256:512] = v[:, 2:4].reshape(256, KC) * mask
        a2[k, 512:640] = v[:, 4].reshape(128, KC) * mask

    def product(h, s, k):
        return lax.dot_general(
            a2[k],
            wb[h, s, k].reshape(256, KC),
            (((1,), (1,)), ((), ())),
            preferred_element_type=F32,
        ).reshape(80, 8, 256)

    for k in range(AHEAD):
        start_first(k)

    wait_first(0)
    prepare(0)
    for ref in sib + own:
        ref[...] = jnp.zeros_like(ref)

    def step_first(k, carry):
        @pl.when(k + AHEAD < NK)
        def _():
            start_first(k + AHEAD)

        @pl.when(k + AHEAD >= NK)
        def _():
            for j in range(4):
                copy_w(1, 0, (k + AHEAD - NK) * 4 + j).start()

        wait_first(k + 1)
        prepare(k + 1)
        sib0[...] += product(0, 0, k)
        own0[...] += product(0, 1, k)
        return carry

    lax.fori_loop(0, NK - 1, step_first, 0)
    for k in range(12, NK):
        copy_w(1, 0, k).start()
    for k in range(NK):
        copy_w(1, 1, k).start()
    sib0[...] += product(0, 0, NK - 1)
    own0[...] += product(0, 1, NK - 1)

    pl.semaphore_wait(barrier, 10)

    def pair(h):
        return pltpu.make_async_remote_copy(
            src_ref=sib[h],
            dst_ref=prt[h],
            send_sem=dsend.at[h],
            recv_sem=drecv.at[h],
            device_id=sibling,
            device_id_type=MESH,
        )

    pair(0).start()

    def group(s, g):
        def step(k, carry):
            copy_w(1, s, k).wait()
            (sib1, own1)[s][...] += product(1, s, k)
            return carry

        lax.fori_loop(g * 5, g * 5 + 5, step, 0)

    def order(p):
        return [(p + j) % 3 for j in range(3)]

    def sems(h, p, stage, d):
        return ((h * 3 + p) * 3 + stage) * 3 + d - 1

    def send(h, p, stage, d):
        axis = order(p)[stage]
        there = lax.rem(place[axis] + d, 4)
        source = S[p].at[h, there] if stage == 0 else T[stage - 1][p].at[h, there]
        n = sems(h, p, stage, d)
        return pltpu.make_async_remote_copy(
            src_ref=source,
            dst_ref=R[stage][p].at[h, d - 1],
            send_sem=ssend.at[n],
            recv_sem=srecv.at[n],
            device_id=peer(axis, d),
            device_id_type=MESH,
        )

    def scatter(h):
        for p in range(3):
            for q in range(32):
                qx, qzh, qy = q // 8, (q // 4) % 2, q % 4
                o = om[q]
                for zl in range(2):
                    lanes = slice(zl * LANES, (zl + 1) * LANES)
                    if p < 2:
                        v = own[h][o + BASE[p], :, lanes] + prt[h][o + BASE[p], :, lanes]
                    else:
                        at = lax.shift_right_logical(o, 1) + BASE[p]
                        v = own[h][at, :, lanes] + prt[h][at, :, lanes]
                        odd = jnp.full((4, LANES), jnp.bitwise_and(o, 1))
                        v = jnp.where(odd == 1, v[4:8], v[0:4])
                    xyz = (qx, qy, qzh * 2 + zl)
                    i1, i2, i3 = (xyz[j] for j in order(p))
                    S[p][h, i1, i2, i3] = v
            for d in (2, 1, 3):
                send(h, p, 0, d).start()

    def collect(h, p, stage):
        axis = order(p)[stage]
        mine = S[p][h, place[axis]] if stage == 0 else T[stage - 1][p][h, place[axis]]
        for d in (1, 3, 2):
            send(h, p, stage, d).wait_recv()
        total = (mine + R[stage][p][h, 0]) + (R[stage][p][h, 1] + R[stage][p][h, 2])
        if stage < 2:
            T[stage][p][h] = total
            for d in (2, 1, 3):
                send(h, p, stage + 1, d).start()
        else:
            lanes = slice(h * LANES, (h + 1) * LANES)
            if p < 2:
                out[2 * p, :, lanes] = total[0:4]
                out[2 * p + 1, :, lanes] = total[4:8]
            else:
                out[4, :, lanes] = total

    group(0, 0)
    group(0, 1)
    group(0, 2)
    pair(1).start()
    pair(0).wait_recv()
    scatter(0)
    group(1, 0)
    group(1, 1)
    group(1, 2)
    pair(1).wait_recv()
    scatter(1)
    for stage in range(3):
        for h in range(2):
            for p in range(3):
                collect(h, p, stage)
    for h in range(2):
        pair(h).wait_send()
        for p in range(3):
            for stage in range(3):
                for d in (1, 2, 3):
                    send(h, p, stage, d).wait_send()


def local(amplitudes, w_vvvo, pair_mask, owner_map):
    w = w_vvvo.reshape(2, 2, 2, LANES, NK * KC)
    smem = pl.BlockSpec(memory_space=pltpu.SMEM)
    hbm = pl.BlockSpec(memory_space=pl.ANY)
    v = pltpu.VMEM
    scratch = [
        v((NK, 160, 4, KC), BF16),
        v((NK, 640, KC), BF16),
        v((2, 2, NK, 2, LANES, KC), BF16),
    ]
    scratch += [v((80, 8, 256), F32)] * 6
    scratch += [v((2, 4, 4, 4, r, LANES), F32) for r in ROWS]
    scratch += [v((2, 3, 4, 4, r, LANES), F32) for r in ROWS]
    scratch += [v((2, 3, 4, r, LANES), F32) for r in ROWS]
    scratch += [v((2, 3, r, LANES), F32) for r in ROWS]
    scratch += [v((2, 4, 4, r, LANES), F32) for r in ROWS]
    scratch += [v((2, 4, r, LANES), F32) for r in ROWS]
    scratch += [
        pltpu.SemaphoreType.DMA((NK,)),
        pltpu.SemaphoreType.DMA((2, 2, NK)),
        pltpu.SemaphoreType.DMA((2,)),
        pltpu.SemaphoreType.DMA((2,)),
        pltpu.SemaphoreType.DMA((54,)),
        pltpu.SemaphoreType.DMA((54,)),
    ]
    return pl.pallas_call(
        kernel,
        out_shape=jax.ShapeDtypeStruct((5, 4, 256), F32),
        in_specs=[smem, smem, hbm, hbm],
        out_specs=pl.BlockSpec(memory_space=pltpu.VMEM),
        scratch_shapes=scratch,
        compiler_params=pltpu.CompilerParams(
            collective_id=0, has_side_effects=True, vmem_limit_bytes=60 * 2**20
        ),
    )(pair_mask, owner_map, amplitudes, w)


def solution(mesh):
    return jax.shard_map(
        local,
        mesh=mesh,
        in_specs=(
            P(None, None, ("grp", "tile")),
            P(None, ("grp", "tile")),
            P(("grp", "tile")),
            P(),
        ),
        out_specs=P("tile", None, "grp"),
        check_vma=False,
    )
```

time: 127 us -> 44.5 us (0.35)
  blocking collectives: 59.6 us -> 0 us
  Pallas kernels: 0 us -> 43 us
  other arithmetic: 24.3 us -> 0 us
  local copies, waits for them, and re-layouts: 24.5 us -> 1.34 us
  matrix products: 16.8 us -> 0 us
    all_to_all x2 -> x0, blocking collectives: 59.6 us -> none  [sent_and_summed(): lax.all_to_all(parts, axis, split_axis=0, concat_axis=0, tiled=True)]
    pallas_call x0 -> x1, Pallas kernels: none -> 43 us  [local(): pl.pallas_call(kernel, out_shape=jax.ShapeDtypeStruct((5, 4, 256), F32),...]
    gather x2 -> x0, other arithmetic: 19.7 us -> none  [the longest x1 19.7 us: shards(): jnp.repeat(pair_mask.astype(jnp.bfloat16), occ_width, total_repeat_length...]
    dot_general x1 -> x0, matrix products: 16.8 us -> none  [full_product(): lax.dot_general(weights, masked, (((1,), (1,)), ((), ())), preferred_elem...]
    reshape x4 -> x0, local copies, waits for them, and re-layouts: 16.6 us -> none  [the longest x1 13.3 us: shards(): amp_flat = amplitudes.reshape(occ_total * root_count, pair_cols)]
    gather x4 -> x0, local copies, waits for them, and re-layouts: 7.02 us -> none  [the longest x2 5.6 us: shards(): jnp.take(term, owner_map, axis=1)]
    select_n x2 -> x0, other arithmetic: 2.97 us -> none  [shards(): jnp.take(term, owner_map, axis=1)]
where the time goes in v1:
time: 44.5 us; the launch traced here: 44.3 us
  Pallas kernels  43 us (97%)
  local copies, waits for them, and re-layouts  1.34 us (3%)
    pallas_call x1, Pallas kernels, local(): pl.pallas_call(kernel, out_shape=jax.ShapeDtypeStruct((5, 4, 256), F32),...  43 us
    unnamed x1, local copies, waits for them, and re-layouts  1.34 us

profile of v1, /device:TPU:0, one launch (start us, length us, event | category | flops | bytes accessed | tf_op | source)
XLA Modules:
  0.0 44.3 jit_solution(6231454116331931010)
XLA Ops:
  0.0 43.0 %shard_map.46 = f32[5,4,256]{2,1,0:T(4,128)} custom-call(s32[32]{0:T(128)} %pm.1, s32[32]{0:T(128)} %om.1, bf16[160,4,7680]{2,1,0:T(4,128)(2,1)} %a_hbm.1, bf16[2,2,2,128,7680]{4,3,2,1,0:T(8,128)(2,1)} %bitcast.1), custom_call_target="tpu_custom_call" | custom-call | tf_op jit(solution)/shard_map/pallas_call | solution.py:261
  43.0 1.3 %copy.6 = f32[5,4,256]{2,1,0:T(4,128)} copy(f32[5,4,256]{2,1,0:T(4,128)} %shard_map.46) | data formatting | bytes 40960

commit v2 on v0

v2 whole, which is shorter than its diff:
```python
import jax
import jax.numpy as jnp
from jax import lax
from jax.experimental import pallas as pl
from jax.experimental.pallas import tpu as pltpu
from jax.sharding import PartitionSpec as P

MESH = pl.DeviceIdType.MESH
F32 = jnp.float32
BF16 = jnp.bfloat16

KC = 512
GROUPS = (1, 2, 3, 4, 3, 2)
STARTS = tuple(sum(GROUPS[:j]) for j in range(len(GROUPS)))
SPLIT = 10
KT = 7680
OCC = 240
BASE = (0, 32, 64)
LANES = 128


def kernel(pm, om, a_hbm, w_hbm, out, *refs):
    n = len(GROUPS)
    a_raw, a2, w0, refs = refs[:n], refs[n : 2 * n], refs[2 * n : 3 * n], refs[3 * n :]
    w1, refs = refs[:3], refs[3:]
    sib, own, prt, refs = refs[:2], refs[2:4], refs[4:6], refs[6:]
    S, R, T, refs = refs[0], refs[1:4], refs[4:6], refs[6:]
    sem_a, sem_w, sem_w1, dsend, drecv, ssend, srecv = refs

    grp = lax.axis_index("grp")
    tile = lax.axis_index("tile")
    core = lax.rem(grp, 2)
    z_lo = grp // 2
    x = tile // 8
    z_hi = lax.rem(tile // 4, 2)
    y = lax.rem(tile, 4)
    place = (x, y, z_hi * 2 + z_lo)

    def peer(axis, d):
        to = list(place)
        to[axis] = lax.rem(to[axis] + d, 4)
        px, py, pz = to
        return (lax.rem(pz, 2) * 2 + core, (px * 2 + pz // 2) * 4 + py)

    sibling = (z_lo * 2 + 1 - core, tile)

    barrier = pltpu.get_barrier_semaphore()
    pl.semaphore_signal(barrier, inc=1, device_id=sibling, device_id_type=MESH)
    for axis in range(3):
        for d in (1, 2, 3):
            pl.semaphore_signal(barrier, inc=1, device_id=peer(axis, d), device_id_type=MESH)

    def columns(first, count):
        return pl.ds(first * KC, count * KC)

    def copies(g):
        cols = columns(STARTS[g], GROUPS[g])
        return (
            pltpu.make_async_copy(a_hbm.at[:, :, cols], a_raw[g], sem_a.at[g]),
            pltpu.make_async_copy(w_hbm.at[:, :, 0, :, cols], w0[g], sem_w.at[g]),
        )

    parts = ((1 - core, 0, SPLIT), (1 - core, SPLIT, 15 - SPLIT), (core, 0, 15))

    def late(j):
        who, first, count = parts[j]
        return pltpu.make_async_copy(
            w_hbm.at[:, who, 1, :, columns(first, count)], w1[j], sem_w1.at[j]
        )

    def prepare(g):
        masks = []
        for k in range(STARTS[g], STARTS[g] + GROUPS[g]):
            first = (k * KC) // OCC
            lane = lax.broadcasted_iota(jnp.int32, (1, KC), 1)
            keep = [pm[min(first + j, 31)] for j in range(4)]
            edge = [OCC * (first + j + 1) - k * KC for j in range(3)]
            row = jnp.where(lane < edge[2], keep[2], keep[3])
            row = jnp.where(lane < edge[0], keep[0], jnp.where(lane < edge[1], keep[1], row))
            masks.append(row.astype(F32).astype(BF16))
        width = GROUPS[g] * KC
        mask = jnp.concatenate(masks, axis=1)
        v = a_raw[g][...].reshape(32, 5, 4, width)
        a2[g][0:256] = v[:, 0:2].reshape(256, width) * mask
        a2[g][256:512] = v[:, 2:4].reshape(256, width) * mask
        a2[g][512:640] = v[:, 4].reshape(128, width) * mask

    def dot(a, w):
        return lax.dot_general(a, w, (((1,), (1,)), ((), ())), preferred_element_type=F32)

    def late_product(j):
        who, first, count = parts[j]
        total = None
        for g in range(n):
            lo, hi = max(first, STARTS[g]), min(first + count, STARTS[g] + GROUPS[g])
            if lo < hi:
                a = a2[g][:, (lo - STARTS[g]) * KC : (hi - STARTS[g]) * KC]
                w = w1[j][:, :, (lo - first) * KC : (hi - first) * KC].reshape(256, (hi - lo) * KC)
                d = dot(a, w)
                total = d if total is None else total + d
        return total.reshape(80, 8, 256)

    def pair(h):
        return pltpu.make_async_remote_copy(
            src_ref=sib[h],
            dst_ref=prt[h],
            send_sem=dsend.at[h],
            recv_sem=drecv.at[h],
            device_id=sibling,
            device_id_type=MESH,
        )

    def order(p):
        return [(p + j) % 3 for j in range(3)]

    def start_stage(h, stage, p):
        axis = order(p)[stage]
        for d in (2, 1, 3):
            there = lax.rem(place[axis] + d, 4)
            pltpu.make_async_remote_copy(
                src_ref=(S if stage == 0 else T[stage - 1]).at[h, p, there],
                dst_ref=R[stage].at[h, p, d - 1],
                send_sem=ssend.at[h * 3 + stage],
                recv_sem=srecv.at[h * 3 + stage],
                device_id=peer(axis, d),
                device_id_type=MESH,
            ).start()

    def whole_stage(h, stage):
        return pltpu.make_async_remote_copy(
            src_ref=R[stage].at[h],
            dst_ref=R[stage].at[h],
            send_sem=ssend.at[h * 3 + stage],
            recv_sem=srecv.at[h * 3 + stage],
            device_id=sibling,
            device_id_type=MESH,
        )

    def pair_sum(h, p):
        for q in range(32):
            qx, qzh, qy = q // 8, (q // 4) % 2, q % 4
            o = om[q]
            for zl in range(2):
                lanes = slice(zl * LANES, (zl + 1) * LANES)
                at = (o if p < 2 else lax.shift_right_logical(o, 1)) + BASE[p]
                v = own[h][at, :, lanes] + prt[h][at, :, lanes]
                if p == 2:
                    odd = jnp.full((8, LANES), jnp.bitwise_and(o, 1))
                    v = jnp.where(odd == 1, jnp.concatenate([v[4:8], v[0:4]], axis=0), v)
                xyz = (qx, qy, qzh * 2 + zl)
                i1, i2, i3 = (xyz[j] for j in order(p))
                S[h, p, i1, i2, i3] = v

    def collect(h, stage):
        whole_stage(h, stage).wait_recv()
        for p in range(3):
            mine = (S if stage == 0 else T[stage - 1])[h, p, place[order(p)[stage]]]
            r = R[stage]
            total = (mine + r[h, p, 0]) + (r[h, p, 1] + r[h, p, 2])
            if stage < 2:
                T[stage][h, p] = total
                start_stage(h, stage + 1, p)
            else:
                lanes = slice(h * LANES, (h + 1) * LANES)
                out[2 * p, :, lanes] = total[0:4]
                if p < 2:
                    out[2 * p + 1, :, lanes] = total[4:8]

    for g in range(n):
        for copy in copies(g):
            copy.start()
    for j in range(3):
        late(j).start()

    for g in range(n):
        for copy in copies(g):
            copy.wait()
        prepare(g)
        for ref, who in ((sib[0], 1 - core), (own[0], core)):
            w = w0[g][:, pl.ds(who, 1)].reshape(256, GROUPS[g] * KC)
            d = dot(a2[g][...], w).reshape(80, 8, 256)
            ref[...] = d if g == 0 else ref[...] + d

    pl.semaphore_wait(barrier, 10)
    pair(0).start()
    late(0).wait()
    sib[1][...] = late_product(0)
    late(1).wait()
    pair(0).wait_recv()
    for p in range(3):
        pair_sum(0, p)
    sib[1][...] += late_product(1)
    pair(1).start()
    for p in range(3):
        start_stage(0, 0, p)
    late(2).wait()
    own[1][...] = late_product(2)
    pair(1).wait_recv()
    for p in range(3):
        pair_sum(1, p)
        start_stage(1, 0, p)
    for stage in range(3):
        for h in range(2):
            collect(h, stage)
    for h in range(2):
        pair(h).wait_send()
        for stage in range(3):
            whole_stage(h, stage).wait_send()


def local(amplitudes, w_vvvo, pair_mask, owner_map):
    w = w_vvvo.reshape(2, 2, 2, LANES, KT)
    smem = pl.BlockSpec(memory_space=pltpu.SMEM)
    hbm = pl.BlockSpec(memory_space=pl.ANY)
    v = pltpu.VMEM
    dma = pltpu.SemaphoreType.DMA
    scratch = [v((160, 4, g * KC), BF16) for g in GROUPS]
    scratch += [v((640, g * KC), BF16) for g in GROUPS]
    scratch += [v((2, 2, LANES, g * KC), BF16) for g in GROUPS]
    scratch += [v((2, LANES, c * KC), BF16) for c in (SPLIT, 15 - SPLIT, 15)]
    scratch += [v((80, 8, 256), F32)] * 6
    scratch += [v((2, 3, 4, 4, 4, 8, LANES), F32)]
    scratch += [v((2, 3, 3, 4, 4, 8, LANES), F32), v((2, 3, 3, 4, 8, LANES), F32)]
    scratch += [v((2, 3, 3, 8, LANES), F32)]
    scratch += [v((2, 3, 4, 4, 8, LANES), F32), v((2, 3, 4, 8, LANES), F32)]
    scratch += [dma((len(GROUPS),)), dma((len(GROUPS),)), dma((3,)), dma((2,)), dma((2,)), dma((6,)), dma((6,))]
    return pl.pallas_call(
        kernel,
        out_shape=jax.ShapeDtypeStruct((5, 4, 256), F32),
        in_specs=[smem, smem, hbm, hbm],
        out_specs=pl.BlockSpec(memory_space=pltpu.VMEM),
        scratch_shapes=scratch,
        compiler_params=pltpu.CompilerParams(
            collective_id=0, has_side_effects=True, vmem_limit_bytes=62 * 2**20
        ),
    )(pair_mask, owner_map, amplitudes, w)


def solution(mesh):
    return jax.shard_map(
        local,
        mesh=mesh,
        in_specs=(
            P(None, None, ("grp", "tile")),
            P(None, ("grp", "tile")),
            P(("grp", "tile")),
            P(),
        ),
        out_specs=P("tile", None, "grp"),
        check_vma=False,
    )
```

time: 127 us -> 39.5 us (0.31)
  blocking collectives: 59.6 us -> 0 us
  Pallas kernels: 0 us -> 38 us
  other arithmetic: 24.3 us -> 0 us
  local copies, waits for them, and re-layouts: 24.5 us -> 1.34 us
  matrix products: 16.8 us -> 0 us
    all_to_all x2 -> x0, blocking collectives: 59.6 us -> none  [sent_and_summed(): lax.all_to_all(parts, axis, split_axis=0, concat_axis=0, tiled=True)]
    pallas_call x0 -> x1, Pallas kernels: none -> 38 us  [local(): pl.pallas_call(kernel, out_shape=jax.ShapeDtypeStruct((5, 4, 256), F32),...]
    gather x2 -> x0, other arithmetic: 19.7 us -> none  [the longest x1 19.7 us: shards(): jnp.repeat(pair_mask.astype(jnp.bfloat16), occ_width, total_repeat_length...]
    dot_general x1 -> x0, matrix products: 16.8 us -> none  [full_product(): lax.dot_general(weights, masked, (((1,), (1,)), ((), ())), preferred_elem...]
    reshape x4 -> x0, local copies, waits for them, and re-layouts: 16.6 us -> none  [the longest x1 13.3 us: shards(): amp_flat = amplitudes.reshape(occ_total * root_count, pair_cols)]
    gather x4 -> x0, local copies, waits for them, and re-layouts: 7.02 us -> none  [the longest x2 5.6 us: shards(): jnp.take(term, owner_map, axis=1)]
    select_n x2 -> x0, other arithmetic: 2.97 us -> none  [shards(): jnp.take(term, owner_map, axis=1)]
where the time goes in v2:
time: 39.5 us; the launch traced here: 39.3 us
  Pallas kernels  38 us (96%)
  local copies, waits for them, and re-layouts  1.34 us (3%)
    pallas_call x1, Pallas kernels, local(): pl.pallas_call(kernel, out_shape=jax.ShapeDtypeStruct((5, 4, 256), F32),...  38 us
    unnamed x1, local copies, waits for them, and re-layouts  1.34 us

profile of v2, /device:TPU:0, one launch (start us, length us, event | category | flops | bytes accessed | tf_op | source)
XLA Modules:
  0.0 39.3 jit_solution(528204582293136938)
XLA Ops:
  0.0 38.0 %shard_map.46 = f32[5,4,256]{2,1,0:T(4,128)} custom-call(s32[32]{0:T(128)} %pm.1, s32[32]{0:T(128)} %om.1, bf16[160,4,7680]{2,1,0:T(4,128)(2,1)} %a_hbm.1, bf16[2,2,2,128,7680]{4,3,2,1,0:T(8,128)(2,1)} %bitcast.1), custom_call_target="tpu_custom_call" | custom-call | tf_op jit(solution)/shard_map/pallas_call | solution.py:227
  38.0 1.3 %copy.6 = f32[5,4,256]{2,1,0:T(4,128)} copy(f32[5,4,256]{2,1,0:T(4,128)} %shard_map.46) | data formatting | bytes 40960

commit v3 on v2

--- a/solution.py
+++ b/solution.py
@@ -12,20 +12,20 @@
 KC = 512
 GROUPS = (1, 2, 3, 4, 3, 2)
 STARTS = tuple(sum(GROUPS[:j]) for j in range(len(GROUPS)))
-SPLIT = 10
+SPLIT = 12
 KT = 7680
 OCC = 240
 BASE = (0, 32, 64)
 LANES = 128
 
 
-def kernel(pm, om, a_hbm, w_hbm, out, *refs):
+def kernel(pm_hbm, om_hbm, a_hbm, w_hbm, out, pm, om, *refs):
     n = len(GROUPS)
     a_raw, a2, w0, refs = refs[:n], refs[n : 2 * n], refs[2 * n : 3 * n], refs[3 * n :]
     w1, refs = refs[:3], refs[3:]
     sib, own, prt, refs = refs[:2], refs[2:4], refs[4:6], refs[6:]
     S, R, T, refs = refs[0], refs[1:4], refs[4:6], refs[6:]
-    sem_a, sem_w, sem_w1, dsend, drecv, ssend, srecv = refs
+    sem_m, sem_a, sem_w, sem_w1, dsend, drecv, ssend, srecv = refs
 
     grp = lax.axis_index("grp")
     tile = lax.axis_index("tile")
@@ -43,12 +43,6 @@
         return (lax.rem(pz, 2) * 2 + core, (px * 2 + pz // 2) * 4 + py)
 
     sibling = (z_lo * 2 + 1 - core, tile)
-
-    barrier = pltpu.get_barrier_semaphore()
-    pl.semaphore_signal(barrier, inc=1, device_id=sibling, device_id_type=MESH)
-    for axis in range(3):
-        for d in (1, 2, 3):
-            pl.semaphore_signal(barrier, inc=1, device_id=peer(axis, d), device_id_type=MESH)
 
     def columns(first, count):
         return pl.ds(first * KC, count * KC)
@@ -88,17 +82,23 @@
     def dot(a, w):
         return lax.dot_general(a, w, (((1,), (1,)), ((), ())), preferred_element_type=F32)
 
-    def late_product(j):
+    def late_product(j, top, bottom):
         who, first, count = parts[j]
         total = None
         for g in range(n):
             lo, hi = max(first, STARTS[g]), min(first + count, STARTS[g] + GROUPS[g])
             if lo < hi:
-                a = a2[g][:, (lo - STARTS[g]) * KC : (hi - STARTS[g]) * KC]
+                a = a2[g][top:bottom, (lo - STARTS[g]) * KC : (hi - STARTS[g]) * KC]
                 w = w1[j][:, :, (lo - first) * KC : (hi - first) * KC].reshape(256, (hi - lo) * KC)
                 d = dot(a, w)
                 total = d if total is None else total + d
-        return total.reshape(80, 8, 256)
+        return total.reshape((bottom - top) // 8, 8, 256)
+
+    def halves(ref, j, more):
+        for top in (0, 320):
+            rows = slice(top // 8, top // 8 + 40)
+            d = late_product(j, top, top + 320)
+            ref[rows] = ref[rows] + d if more else d
 
     def pair(h):
         return pltpu.make_async_remote_copy(
@@ -166,11 +166,26 @@
                 if p < 2:
                     out[2 * p + 1, :, lanes] = total[4:8]
 
+    tables = (
+        pltpu.make_async_copy(pm_hbm, pm, sem_m.at[0]),
+        pltpu.make_async_copy(om_hbm, om, sem_m.at[1]),
+    )
+    for copy in tables:
+        copy.start()
     for g in range(n):
         for copy in copies(g):
             copy.start()
     for j in range(3):
         late(j).start()
+
+    barrier = pltpu.get_barrier_semaphore()
+    pl.semaphore_signal(barrier, inc=1, device_id=sibling, device_id_type=MESH)
+    for axis in range(3):
+        for d in (1, 2, 3):
+            pl.semaphore_signal(barrier, inc=1, device_id=peer(axis, d), device_id_type=MESH)
+
+    for copy in tables:
+        copy.wait()
 
     for g in range(n):
         for copy in copies(g):
@@ -184,17 +199,17 @@
     pl.semaphore_wait(barrier, 10)
     pair(0).start()
     late(0).wait()
-    sib[1][...] = late_product(0)
+    halves(sib[1], 0, False)
     late(1).wait()
     pair(0).wait_recv()
     for p in range(3):
         pair_sum(0, p)
-    sib[1][...] += late_product(1)
+    halves(sib[1], 1, True)
     pair(1).start()
     for p in range(3):
         start_stage(0, 0, p)
     late(2).wait()
-    own[1][...] = late_product(2)
+    halves(own[1], 2, False)
     pair(1).wait_recv()
     for p in range(3):
         pair_sum(1, p)
@@ -210,11 +225,11 @@
 
 def local(amplitudes, w_vvvo, pair_mask, owner_map):
     w = w_vvvo.reshape(2, 2, 2, LANES, KT)
-    smem = pl.BlockSpec(memory_space=pltpu.SMEM)
     hbm = pl.BlockSpec(memory_space=pl.ANY)
     v = pltpu.VMEM
     dma = pltpu.SemaphoreType.DMA
-    scratch = [v((160, 4, g * KC), BF16) for g in GROUPS]
+    scratch = [pltpu.SMEM((32,), jnp.int32)] * 2
+    scratch += [v((160, 4, g * KC), BF16) for g in GROUPS]
     scratch += [v((640, g * KC), BF16) for g in GROUPS]
     scratch += [v((2, 2, LANES, g * KC), BF16) for g in GROUPS]
     scratch += [v((2, LANES, c * KC), BF16) for c in (SPLIT, 15 - SPLIT, 15)]
@@ -223,11 +238,11 @@
     scratch += [v((2, 3, 3, 4, 4, 8, LANES), F32), v((2, 3, 3, 4, 8, LANES), F32)]
     scratch += [v((2, 3, 3, 8, LANES), F32)]
     scratch += [v((2, 3, 4, 4, 8, LANES), F32), v((2, 3, 4, 8, LANES), F32)]
-    scratch += [dma((len(GROUPS),)), dma((len(GROUPS),)), dma((3,)), dma((2,)), dma((2,)), dma((6,)), dma((6,))]
+    scratch += [dma((2,)), dma((len(GROUPS),)), dma((len(GROUPS),)), dma((3,)), dma((2,)), dma((2,)), dma((6,)), dma((6,))]
     return pl.pallas_call(
         kernel,
-        out_shape=jax.ShapeDtypeStruct((5, 4, 256), F32),
-        in_specs=[smem, smem, hbm, hbm],
+        out_shape=pltpu.VMEM((5, 4, 256), F32),
+        in_specs=[hbm] * 4,
         out_specs=pl.BlockSpec(memory_space=pltpu.VMEM),
         scratch_shapes=scratch,
         compiler_params=pltpu.CompilerParams(

time: 39.5 us -> 32.4 us (0.82)
  Pallas kernels: 38 us -> 31.6 us
  local copies, waits for them, and re-layouts: 1.34 us -> 0.61 us
    pallas_call x1, Pallas kernels: 38 us -> 31.6 us  [local(): pl.pallas_call(kernel, out_shape=pltpu.VMEM((5, 4, 256), F32), in_specs=[...]
    unnamed x1, local copies, waits for them, and re-layouts: 1.34 us -> 0.61 us
where the time goes in v3:
time: 32.4 us; the launch traced here: 32.3 us
  Pallas kernels  31.6 us (98%)
  local copies, waits for them, and re-layouts  0.61 us (2%)
    pallas_call x1, Pallas kernels, local(): pl.pallas_call(kernel, out_shape=pltpu.VMEM((5, 4, 256), F32), in_specs=[...  31.6 us

profile of v3, /device:TPU:0, one launch (start us, length us, event | category | flops | bytes accessed | tf_op | source)
XLA Modules:
  0.0 32.3 jit_solution(13266132813350244070)
XLA Ops:
  0.0 31.6 %shard_map.46 = f32[5,4,256]{2,1,0:T(4,128)S(1)} custom-call(s32[32]{0:T(128)} %pm_hbm.1, s32[32]{0:T(128)} %om_hbm.1, bf16[160,4,7680]{2,1,0:T(4,128)(2,1)} %a_hbm.1, bf16[2,2,2,128,7680]{4,3,2,1,0:T(8,128)(2,1)} %bitcast.1), custom_call_target="tpu_custom_call" | custom-call | tf_op jit(solution)/shard_map/pallas_call | solution.py:242
  31.7 0.6 %copy.6 = f32[5,4,256]{2,1,0:T(4,128)} copy(f32[5,4,256]{2,1,0:T(4,128)S(1)} %shard_map.46) | data formatting | bytes 40960

commit v4 on v3

--- a/solution.py
+++ b/solution.py
@@ -24,7 +24,7 @@
     a_raw, a2, w0, refs = refs[:n], refs[n : 2 * n], refs[2 * n : 3 * n], refs[3 * n :]
     w1, refs = refs[:3], refs[3:]
     sib, own, prt, refs = refs[:2], refs[2:4], refs[4:6], refs[6:]
-    S, R, T, refs = refs[0], refs[1:4], refs[4:6], refs[6:]
+    S, R, T, plane, refs = refs[0], refs[1:4], refs[4:6], refs[6], refs[7:]
     sem_m, sem_a, sem_w, sem_w1, dsend, drecv, ssend, srecv = refs
 
     grp = lax.axis_index("grp")
@@ -36,9 +36,10 @@
     y = lax.rem(tile, 4)
     place = (x, y, z_hi * 2 + z_lo)
 
-    def peer(axis, d):
+    def peer(*moves):
         to = list(place)
-        to[axis] = lax.rem(to[axis] + d, 4)
+        for axis, d in moves:
+            to[axis] = lax.rem(to[axis] + d, 4)
         px, py, pz = to
         return (lax.rem(pz, 2) * 2 + core, (px * 2 + pz // 2) * 4 + py)
 
@@ -122,7 +123,7 @@
                 dst_ref=R[stage].at[h, p, d - 1],
                 send_sem=ssend.at[h * 3 + stage],
                 recv_sem=srecv.at[h * 3 + stage],
-                device_id=peer(axis, d),
+                device_id=peer((axis, d)),
                 device_id_type=MESH,
             ).start()
 
@@ -151,6 +152,45 @@
                 i1, i2, i3 = (xyz[j] for j in order(p))
                 S[h, p, i1, i2, i3] = v
 
+    def start_plane(p):
+        _, b, c = order(p)
+        for d in sorted(range(1, 16), key=lambda d: -(2 - abs(d // 4 - 2)) - (2 - abs(d % 4 - 2))):
+            e, f = d // 4, d % 4
+            source = T[0].at[1, p, lax.rem(place[b] + e, 4), lax.rem(place[c] + f, 4)]
+            pltpu.make_async_remote_copy(
+                src_ref=source,
+                dst_ref=plane.at[p, d - 1],
+                send_sem=ssend.at[4],
+                recv_sem=srecv.at[4],
+                device_id=peer(*[m for m in ((b, e), (c, f)) if m[1]]),
+                device_id_type=MESH,
+            ).start()
+
+    def whole_plane():
+        return pltpu.make_async_remote_copy(
+            src_ref=plane,
+            dst_ref=plane,
+            send_sem=ssend.at[4],
+            recv_sem=srecv.at[4],
+            device_id=sibling,
+            device_id_type=MESH,
+        )
+
+    def finish(h, p, total):
+        lanes = slice(h * LANES, (h + 1) * LANES)
+        out[2 * p, :, lanes] = total[0:4]
+        if p < 2:
+            out[2 * p + 1, :, lanes] = total[4:8]
+
+    def collect_plane():
+        whole_plane().wait_recv()
+        for p in range(3):
+            _, b, c = order(p)
+            terms = [T[0][1, p, place[b], place[c]]] + [plane[p, j] for j in range(15)]
+            while len(terms) > 1:
+                terms = [u + w for u, w in zip(terms[::2], terms[1::2])]
+            finish(1, p, terms[0])
+
     def collect(h, stage):
         whole_stage(h, stage).wait_recv()
         for p in range(3):
@@ -159,12 +199,12 @@
             total = (mine + r[h, p, 0]) + (r[h, p, 1] + r[h, p, 2])
             if stage < 2:
                 T[stage][h, p] = total
-                start_stage(h, stage + 1, p)
+                if h == 0:
+                    start_stage(h, stage + 1, p)
+                else:
+                    start_plane(p)
             else:
-                lanes = slice(h * LANES, (h + 1) * LANES)
-                out[2 * p, :, lanes] = total[0:4]
-                if p < 2:
-                    out[2 * p + 1, :, lanes] = total[4:8]
+                finish(h, p, total)
 
     tables = (
         pltpu.make_async_copy(pm_hbm, pm, sem_m.at[0]),
@@ -182,7 +222,9 @@
     pl.semaphore_signal(barrier, inc=1, device_id=sibling, device_id_type=MESH)
     for axis in range(3):
         for d in (1, 2, 3):
-            pl.semaphore_signal(barrier, inc=1, device_id=peer(axis, d), device_id_type=MESH)
+            for e in range(4):
+                to = peer((axis, d), ((axis + 1) % 3, e)) if e else peer((axis, d))
+                pl.semaphore_signal(barrier, inc=1, device_id=to, device_id_type=MESH)
 
     for copy in tables:
         copy.wait()
@@ -196,7 +238,7 @@
             d = dot(a2[g][...], w).reshape(80, 8, 256)
             ref[...] = d if g == 0 else ref[...] + d
 
-    pl.semaphore_wait(barrier, 10)
+    pl.semaphore_wait(barrier, 37)
     pair(0).start()
     late(0).wait()
     halves(sib[1], 0, False)
@@ -214,13 +256,18 @@
     for p in range(3):
         pair_sum(1, p)
         start_stage(1, 0, p)
-    for stage in range(3):
-        for h in range(2):
-            collect(h, stage)
-    for h in range(2):
-        pair(h).wait_send()
-        for stage in range(3):
-            whole_stage(h, stage).wait_send()
+    collect(0, 0)
+    collect(1, 0)
+    collect(0, 1)
+    pair(0).wait_send()
+    pair(1).wait_send()
+    whole_stage(0, 0).wait_send()
+    whole_stage(1, 0).wait_send()
+    whole_stage(0, 1).wait_send()
+    collect(0, 2)
+    collect_plane()
+    whole_stage(0, 2).wait_send()
+    whole_plane().wait_send()
 
 
 def local(amplitudes, w_vvvo, pair_mask, owner_map):
@@ -238,6 +285,7 @@
     scratch += [v((2, 3, 3, 4, 4, 8, LANES), F32), v((2, 3, 3, 4, 8, LANES), F32)]
     scratch += [v((2, 3, 3, 8, LANES), F32)]
     scratch += [v((2, 3, 4, 4, 8, LANES), F32), v((2, 3, 4, 8, LANES), F32)]
+    scratch += [v((3, 15, 8, LANES), F32)]
     scratch += [dma((2,)), dma((len(GROUPS),)), dma((len(GROUPS),)), dma((3,)), dma((2,)), dma((2,)), dma((6,)), dma((6,))]
     return pl.pallas_call(
         kernel,

time: 32.4 us -> 30.7 us (0.948)
  Pallas kernels: 31.6 us -> 29.8 us
    pallas_call x1, Pallas kernels: 31.6 us -> 29.8 us  [local(): pl.pallas_call(kernel, out_shape=pltpu.VMEM((5, 4, 256), F32), in_specs=[...]
where the time goes in v4:
time: 30.7 us; the launch traced here: 30.4 us
  Pallas kernels  29.8 us (97%)
  local copies, waits for them, and re-layouts  0.61 us (2%)
    pallas_call x1, Pallas kernels, local(): pl.pallas_call(kernel, out_shape=pltpu.VMEM((5, 4, 256), F32), in_specs=[...  29.8 us

profile of v4, /device:TPU:0, one launch (start us, length us, event | category | flops | bytes accessed | tf_op | source)
XLA Modules:
  0.0 30.4 jit_solution(2390778068831536326)
XLA Ops:
  0.0 29.8 %shard_map.46 = f32[5,4,256]{2,1,0:T(4,128)S(1)} custom-call(s32[32]{0:T(128)} %pm_hbm.1, s32[32]{0:T(128)} %om_hbm.1, bf16[160,4,7680]{2,1,0:T(4,128)(2,1)} %a_hbm.1, bf16[2,2,2,128,7680]{4,3,2,1,0:T(8,128)(2,1)} %bitcast.1), custom_call_target="tpu_custom_call" | custom-call | tf_op jit(solution)/shard_map/pallas_call | solution.py:290
  29.8 0.6 %copy.6 = f32[5,4,256]{2,1,0:T(4,128)} copy(f32[5,4,256]{2,1,0:T(4,128)S(1)} %shard_map.46) | data formatting | bytes 40960

commit v5 on v4

--- a/solution.py
+++ b/solution.py
@@ -10,7 +10,7 @@
 BF16 = jnp.bfloat16
 
 KC = 512
-GROUPS = (1, 2, 3, 4, 3, 2)
+GROUPS = (1, 1, 2, 2, 3, 3, 2, 1)
 STARTS = tuple(sum(GROUPS[:j]) for j in range(len(GROUPS)))
 SPLIT = 12
 KT = 7680
@@ -121,18 +121,18 @@
             pltpu.make_async_remote_copy(
                 src_ref=(S if stage == 0 else T[stage - 1]).at[h, p, there],
                 dst_ref=R[stage].at[h, p, d - 1],
-                send_sem=ssend.at[h * 3 + stage],
-                recv_sem=srecv.at[h * 3 + stage],
+                send_sem=ssend.at[h * 9 + stage * 3 + p],
+                recv_sem=srecv.at[h * 9 + stage * 3 + p],
                 device_id=peer((axis, d)),
                 device_id_type=MESH,
             ).start()
 
-    def whole_stage(h, stage):
+    def whole_stage(h, stage, p):
         return pltpu.make_async_remote_copy(
-            src_ref=R[stage].at[h],
-            dst_ref=R[stage].at[h],
-            send_sem=ssend.at[h * 3 + stage],
-            recv_sem=srecv.at[h * 3 + stage],
+            src_ref=R[stage].at[h, p],
+            dst_ref=R[stage].at[h, p],
+            send_sem=ssend.at[h * 9 + stage * 3 + p],
+            recv_sem=srecv.at[h * 9 + stage * 3 + p],
             device_id=sibling,
             device_id_type=MESH,
         )
@@ -160,18 +160,18 @@
             pltpu.make_async_remote_copy(
                 src_ref=source,
                 dst_ref=plane.at[p, d - 1],
-                send_sem=ssend.at[4],
-                recv_sem=srecv.at[4],
+                send_sem=ssend.at[12 + p],
+                recv_sem=srecv.at[12 + p],
                 device_id=peer(*[m for m in ((b, e), (c, f)) if m[1]]),
                 device_id_type=MESH,
             ).start()
 
-    def whole_plane():
+    def whole_plane(p):
         return pltpu.make_async_remote_copy(
-            src_ref=plane,
-            dst_ref=plane,
-            send_sem=ssend.at[4],
-            recv_sem=srecv.at[4],
+            src_ref=plane.at[p],
+            dst_ref=plane.at[p],
+            send_sem=ssend.at[12 + p],
+            recv_sem=srecv.at[12 + p],
             device_id=sibling,
             device_id_type=MESH,
         )
@@ -183,8 +183,8 @@
             out[2 * p + 1, :, lanes] = total[4:8]
 
     def collect_plane():
-        whole_plane().wait_recv()
         for p in range(3):
+            whole_plane(p).wait_recv()
             _, b, c = order(p)
             terms = [T[0][1, p, place[b], place[c]]] + [plane[p, j] for j in range(15)]
             while len(terms) > 1:
@@ -192,8 +192,8 @@
             finish(1, p, terms[0])
 
     def collect(h, stage):
-        whole_stage(h, stage).wait_recv()
         for p in range(3):
+            whole_stage(h, stage, p).wait_recv()
             mine = (S if stage == 0 else T[stage - 1])[h, p, place[order(p)[stage]]]
             r = R[stage]
             total = (mine + r[h, p, 0]) + (r[h, p, 1] + r[h, p, 2])
@@ -261,13 +261,14 @@
     collect(0, 1)
     pair(0).wait_send()
     pair(1).wait_send()
-    whole_stage(0, 0).wait_send()
-    whole_stage(1, 0).wait_send()
-    whole_stage(0, 1).wait_send()
+    for h, stage in ((0, 0), (1, 0), (0, 1)):
+        for p in range(3):
+            whole_stage(h, stage, p).wait_send()
     collect(0, 2)
     collect_plane()
-    whole_stage(0, 2).wait_send()
-    whole_plane().wait_send()
+    for p in range(3):
+        whole_stage(0, 2, p).wait_send()
+        whole_plane(p).wait_send()
 
 
 def local(amplitudes, w_vvvo, pair_mask, owner_map):
@@ -286,7 +287,7 @@
     scratch += [v((2, 3, 3, 8, LANES), F32)]
     scratch += [v((2, 3, 4, 4, 8, LANES), F32), v((2, 3, 4, 8, LANES), F32)]
     scratch += [v((3, 15, 8, LANES), F32)]
-    scratch += [dma((2,)), dma((len(GROUPS),)), dma((len(GROUPS),)), dma((3,)), dma((2,)), dma((2,)), dma((6,)), dma((6,))]
+    scratch += [dma((2,)), dma((len(GROUPS),)), dma((len(GROUPS),)), dma((3,)), dma((2,)), dma((2,)), dma((18,)), dma((18,))]
     return pl.pallas_call(
         kernel,
         out_shape=pltpu.VMEM((5, 4, 256), F32),

time: 30.7 us -> 30 us (0.977)
  Pallas kernels: 29.8 us -> 29.3 us
    pallas_call x1, Pallas kernels: 29.8 us -> 29.3 us  [local(): pl.pallas_call(kernel, out_shape=pltpu.VMEM((5, 4, 256), F32), in_specs=[...]
where the time goes in v5:
time: 30 us; the launch traced here: 29.9 us
  Pallas kernels  29.3 us (98%)
  local copies, waits for them, and re-layouts  0.61 us (2%)
    pallas_call x1, Pallas kernels, local(): pl.pallas_call(kernel, out_shape=pltpu.VMEM((5, 4, 256), F32), in_specs=[...  29.3 us
    unnamed x1, local copies, waits for them, and re-layouts  0.61 us

profile of v5, /device:TPU:0, one launch (start us, length us, event | category | flops | bytes accessed | tf_op | source)
XLA Modules:
  0.0 29.9 jit_solution(6609027329977292009)
XLA Ops:
  0.0 29.3 %shard_map.46 = f32[5,4,256]{2,1,0:T(4,128)S(1)} custom-call(s32[32]{0:T(128)} %pm_hbm.1, s32[32]{0:T(128)} %om_hbm.1, bf16[160,4,7680]{2,1,0:T(4,128)(2,1)} %a_hbm.1, bf16[2,2,2,128,7680]{4,3,2,1,0:T(8,128)(2,1)} %bitcast.1), custom_call_target="tpu_custom_call" | custom-call | tf_op jit(solution)/shard_map/pallas_call | solution.py:291
  29.3 0.6 %copy.6 = f32[5,4,256]{2,1,0:T(4,128)} copy(f32[5,4,256]{2,1,0:T(4,128)S(1)} %shard_map.46) | data formatting | bytes 40960

commit v6 on v5

--- a/solution.py
+++ b/solution.py
@@ -264,8 +264,8 @@
     for h, stage in ((0, 0), (1, 0), (0, 1)):
         for p in range(3):
             whole_stage(h, stage, p).wait_send()
+    collect_plane()
     collect(0, 2)
-    collect_plane()
     for p in range(3):
         whole_stage(0, 2, p).wait_send()
         whole_plane(p).wait_send()

time: 30 us -> 30.1 us (level)
  no operation moved by 1% of the time
where the time goes in v6:
time: 30.1 us; the launch traced here: 30 us
  Pallas kernels  29.4 us (98%)
  local copies, waits for them, and re-layouts  0.61 us (2%)
    pallas_call x1, Pallas kernels, local(): pl.pallas_call(kernel, out_shape=pltpu.VMEM((5, 4, 256), F32), in_specs=[...  29.4 us
    unnamed x1, local copies, waits for them, and re-layouts  0.61 us

profile of v6, /device:TPU:0, one launch (start us, length us, event | category | flops | bytes accessed | tf_op | source)
XLA Modules:
  0.0 30.0 jit_solution(13860061435105466070)
XLA Ops:
  0.0 29.4 %shard_map.46 = f32[5,4,256]{2,1,0:T(4,128)S(1)} custom-call(s32[32]{0:T(128)} %pm_hbm.1, s32[32]{0:T(128)} %om_hbm.1, bf16[160,4,7680]{2,1,0:T(4,128)(2,1)} %a_hbm.1, bf16[2,2,2,128,7680]{4,3,2,1,0:T(8,128)(2,1)} %bitcast.1), custom_call_target="tpu_custom_call" | custom-call | tf_op jit(solution)/shard_map/pallas_call | solution.py:291
  29.4 0.6 %copy.6 = f32[5,4,256]{2,1,0:T(4,128)} copy(f32[5,4,256]{2,1,0:T(4,128)S(1)} %shard_map.46) | data formatting | bytes 40960
